TPU v7x, 32 devices: a whole 2x2x4 slice. The times are simulated.
32 devices in a mesh: row: 4 (over y, x), col: 4 (over z), depth: 2 (over core).
Axes of the slice: x: 2, y: 2, z: 4, core: 2. Of those that a mesh axis runs over, the one named last changes fastest.
Arguments:
- orbitals: bfloat16 [2, 1024, 2, 4096], P(None, ('row', 'col'), 'depth'), may hold values from -20 to 20
- potential: float32 [2, 4096], P('depth'), may hold values from -6 to 6
Outputs:
- intersection: float32 [1024, 2, 1024], P(('row', 'depth'), None, 'col')
- applied: bfloat16 [2, 1024, 2, 4096], P(None, ('row', 'col'), 'depth')
All inputs are finite; a program needn't handle non-finite values.
Results may differ from a plain program's by a relative error of at most 0.001.
Values may be sent and summed in bfloat16 or wider, within the bound.
A program may use at most 128 MiB of HBM per device.

v0:
```python
import functools

import jax
import jax.numpy as jnp
from jax import lax
from jax.experimental import pallas as pl
from jax.experimental.pallas import tpu as pltpu
from jax.sharding import PartitionSpec as P

NX = 64
MESH = pl.DeviceIdType.MESH


def with_halo(block, sides, width):
    for axis, dim in sides:
        count = lax.axis_size(axis)
        forward = [(i, i + 1) for i in range(count - 1)]
        forward.append((count - 1, 0))
        backward = [(target, source) for source, target in forward]
        low = lax.ppermute(
            lax.slice_in_dim(block, block.shape[dim] - width, None, axis=dim), axis, forward
        )
        high = lax.ppermute(lax.slice_in_dim(block, 0, width, axis=dim), axis, backward)
        block = jnp.concatenate([low, block, high], axis=dim)
    return block


def apply_operator(padded, potential):
    center = padded[:, :, 1:-1].astype(jnp.float32)
    below = padded[:, :, :-2].astype(jnp.float32)
    above = padded[:, :, 2:].astype(jnp.float32)
    flat_cells = center.shape[-1]
    xpos = jnp.arange(flat_cells) % NX
    yminus = jnp.roll(center, NX, axis=3)
    yplus = jnp.roll(center, -NX, axis=3)
    xminus = jnp.where(xpos == 0, jnp.roll(center, 1 - NX, axis=3), jnp.roll(center, 1, axis=3))
    xplus = jnp.where(
        xpos == NX - 1, jnp.roll(center, NX - 1, axis=3), jnp.roll(center, -1, axis=3)
    )
    lap = below + above + yminus + yplus + xminus + xplus - 6.0 * center
    return (-0.5 * lap + potential[None, None] * center).astype(jnp.bfloat16)


def contract(left, right):
    return lax.dot_general(
        left, right, (((1,), (1,)), ((), ())), preferred_element_type=jnp.float32
    )


def shards(orbitals, potential):
    parts, orbs, planes, cells = orbitals.shape
    flat = orbitals.reshape(parts, orbs, planes * cells)
    panel = lax.all_gather(flat, "col", axis=1, tiled=True)
    other = lax.all_gather(flat, "row", axis=1, tiled=True)
    padded = with_halo(orbitals, (("depth", 2),), 1)
    applied = apply_operator(padded, potential)
    dvol = 1.0 / (planes * lax.axis_size("depth") * cells)
    tile_cols = other.shape[1]
    real_rows = panel[0]
    imag_rows = panel[1]
    sreal = contract(real_rows, other[0]) + contract(imag_rows, other[1])
    simag = contract(real_rows, other[1]) - contract(imag_rows, other[0])
    summed = lax.psum_scatter(
        dvol * jnp.concatenate([sreal, simag], axis=1), "depth", scatter_dimension=0, tiled=True
    )
    intersection = summed.reshape(summed.shape[0], 2, tile_cols)
    intersection = lax.all_to_all(intersection, "col", split_axis=2, concat_axis=2, tiled=True)
    return (intersection, applied)


def flip(a, b):
    low = lax.rem(lax.rem(a, 2) + lax.rem(b, 2), 2)
    high = lax.rem(lax.div(a, 2) + lax.div(b, 2), 2)
    return 2 * high + low


def stencil(orb, halo, pot, out):
    parts, orbs, cells = orb.shape
    step = 16
    xpos = lax.broadcasted_iota(jnp.int32, (step, cells), 1) % NX
    first, last = xpos == 0, xpos == NX - 1

    def body(i, carry):
        part = lax.div(i, orbs // step)
        rows = pl.ds(pl.multiple_of(lax.rem(i, orbs // step) * step, step), step)
        center = orb[part, rows, :].astype(jnp.float32)
        side = halo[part, rows, :].astype(jnp.float32)
        right = pltpu.roll(center, 1, 1)
        left = pltpu.roll(center, cells - 1, 1)
        yminus = pltpu.roll(center, NX, 1)
        yplus = pltpu.roll(center, cells - NX, 1)
        xminus = jnp.where(first, pltpu.roll(right, cells - NX, 1), right)
        xplus = jnp.where(last, pltpu.roll(left, NX, 1), left)
        lap = side + side + yminus + yplus + xminus + xplus - 6.0 * center
        out[part, rows, :] = (-0.5 * lap + pot[0:1, :] * center).astype(out.dtype)
        return carry

    lax.fori_loop(0, parts * (orbs // step), body, 0)


def kernel(dvol, orb_hbm, pot_hbm, inter, applied, orb, pot, halo, panel, acc, give, take,
           land, relay, ins, hs, hr, ls, zs, zr, xs, xr, ds, dr, gs, gr, qr, rs, rr):
    r, c, d = lax.axis_index("row"), lax.axis_index("col"), lax.axis_index("depth")
    parts, orbs, cells = orb.shape
    quarter = cells // 4
    half = acc.shape[2]
    load = pltpu.make_async_copy(orb_hbm, orb, ins.at[0])
    load.start()
    load_pot = pltpu.make_async_copy(pot_hbm, pot, ins.at[1])
    load_pot.start()
    peer = (r, c, 1 - d)
    zdev = [None] + [(r, flip(c, k), d) for k in (1, 2, 3)]
    xdev = [None] + [(flip(r, k), c, d) for k in (1, 2)]

    barrier = pltpu.get_barrier_semaphore()
    friends = [peer] + zdev[1:] + xdev[1:]
    for dev in friends:
        pl.semaphore_signal(barrier, inc=1, device_id=dev, device_id_type=MESH)
    load.wait()
    pl.semaphore_wait(barrier, len(friends))

    def send(src, dst, ssem, rsem, dev):
        return pltpu.make_async_remote_copy(
            src_ref=src, dst_ref=dst, send_sem=ssem, recv_sem=rsem,
            device_id=dev, device_id_type=MESH,
        )

    def lanes(k):
        return pl.ds(pl.multiple_of(k * quarter, quarter), quarter)

    def block(j, k, part):
        return panel.at[j, part, pl.ds(pl.multiple_of(k * orbs, orbs), orbs), :]

    zsend, xsend = {}, {}
    for k in (1, 3, 2):
        for p in (0, 1):
            zsend[k, p] = send(orb.at[p, :, lanes(flip(c, k))], block(0, c, p),
                               zs.at[k, p], zr.at[k, p], zdev[k])
            zsend[k, p].start()
    for p in (0, 1):
        for j in (1, 2):
            xsend[0, j, p] = send(orb.at[p, :, lanes(c)], block(j, c, p),
                                  xs.at[0, j, p], xr.at[0, j, p], xdev[j])
            xsend[0, j, p].start()
    edge = send(orb, halo, hs, hr, peer)
    edge.start()
    local = [pltpu.make_async_copy(orb.at[p, :, lanes(c)], block(0, c, p), ls.at[p])
             for p in (0, 1)]
    for cp in local:
        cp.start()

    load_pot.wait()
    edge.wait()
    stencil(orb, halo, pot, applied)
    for cp in local:
        cp.wait()

    for k in (1, 3, 2):
        for p in (0, 1):
            zsend[k, p].wait_recv()
            for j in (1, 2):
                xsend[k, j, p] = send(block(0, flip(c, k), p), block(j, flip(c, k), p),
                                      xs.at[k, j, p], xr.at[k, j, p], xdev[j])
                xsend[k, j, p].start()

    def tile(slot, jl, jr):
        for part in (0, 1):
            if slot == 4 and part == 1:
                jl, jr = jr, jl
            a, b = panel[jl, 0], panel[jl, 1]
            if part == 0:
                s = contract(a, panel[jr, 0]) + contract(b, panel[jr, 1])
            else:
                s = contract(a, panel[jr, 1]) - contract(b, panel[jr, 0])
            acc[slot, part] = jnp.where(d == 0, s[:half], s[half:])
            give[slot, part] = jnp.where(d == 0, s[half:], s[:half])
        cp = send(give.at[slot], take.at[slot], ds.at[slot], dr.at[slot], peer)
        cp.start()
        return cp

    inner = lax.rem(c + 1, 4) >= 2

    def ship(t):
        to = flip(r, jnp.int32(t))
        return to, lax.div(to, 2) != lax.div(c, 2)

    def start_ship(t):
        to, across = ship(t)

        @pl.when(jnp.logical_and(to != c, jnp.logical_not(across)))
        def _():
            send(acc.at[t], land.at[0], gs.at[t], gr.at[0], zdev[1]).start()

        @pl.when(jnp.logical_and(across, jnp.logical_not(inner)))
        def _():
            send(acc.at[t], relay.at[t], gs.at[t], qr.at[t], zdev[1]).start()

    def pass_on(t):
        to, across = ship(t)

        @pl.when(jnp.logical_and(across, inner))
        def _():
            send(acc.at[t], relay.at[t], gs.at[t], qr.at[t], zdev[1]).wait_recv()
            acc[t] += relay[t]
            send(acc.at[t], land.at[1], gs.at[t], gr.at[1], (r, to, d)).start()

    def settle(t):
        pair[t].wait_recv()
        acc[t] += take[t]

    pair = {0: tile(0, 0, 0)}
    settle(0)
    start_ship(0)
    for k in (0, 1, 3, 2):
        for j in (1, 2):
            for p in (0, 1):
                xsend[k, j, p].wait_recv()
    pair[4] = tile(4, 1, 2)
    pair[2] = tile(2, 0, 2)
    settle(4)
    cross = [send(acc.at[4, p], acc.at[3, p], rs.at[p], rr.at[p], xdev[1 + p]) for p in (0, 1)]
    for cp in cross:
        cp.start()
    settle(2)
    start_ship(2)
    pair[1] = tile(1, 0, 1)
    pass_on(0)
    settle(1)
    for cp in cross:
        cp.wait_recv()
    start_ship(3)
    start_ship(1)
    pass_on(2)
    pass_on(3)
    pass_on(1)

    total = acc[flip(r, c)]
    for k in (0, 1):
        send(acc.at[0], land.at[k], gs.at[0], gr.at[k], zdev[1]).wait_recv()
        total = total + land[k]
    inter[...] = total * dvol

    for cp in [edge] + cross + list(pair.values()) + list(zsend.values()) + list(xsend.values()):
        if cp is not edge:
            cp.wait_send()
    for t in (0, 1, 2, 3):
        to, across = ship(t)

        @pl.when(to != c)
        def _():
            send(acc.at[t], land.at[0], gs.at[t], gr.at[0], zdev[1]).wait_send()


def exchange(orbitals, potential):
    parts, orbs, planes, cells = orbitals.shape
    rows = orbs * lax.axis_size("col")
    half = rows // 2
    dvol = 1.0 / (planes * lax.axis_size("depth") * cells)
    vmem = pl.BlockSpec(memory_space=pltpu.VMEM)
    dma = pltpu.SemaphoreType.DMA
    inter, applied = pl.pallas_call(
        functools.partial(kernel, dvol),
        out_shape=(
            jax.ShapeDtypeStruct((2, half, rows), jnp.float32),
            jax.ShapeDtypeStruct((parts, orbs, cells), jnp.bfloat16),
        ),
        in_specs=[pl.BlockSpec(memory_space=pltpu.HBM)] * 2,
        out_specs=(vmem, vmem),
        scratch_shapes=[
            pltpu.VMEM((parts, orbs, cells), jnp.bfloat16),
            pltpu.VMEM(potential.shape, jnp.float32),
            pltpu.VMEM((parts, orbs, cells), jnp.bfloat16),
            pltpu.VMEM((3, parts, rows, cells // 4), jnp.bfloat16),
            pltpu.VMEM((5, 2, half, rows), jnp.float32),
            pltpu.VMEM((5, 2, half, rows), jnp.float32),
            pltpu.VMEM((5, 2, half, rows), jnp.float32),
            pltpu.VMEM((2, 2, half, rows), jnp.float32),
            pltpu.VMEM((4, 2, half, rows), jnp.float32),
            dma((2,)), dma, dma, dma((2,)), dma((4, 2)), dma((4, 2)), dma((4, 3, 2)),
            dma((4, 3, 2)), dma((5,)), dma((5,)), dma((4,)), dma((2,)), dma((4,)), dma((2,)), dma((2,)),
        ],
        compiler_params=pltpu.CompilerParams(
            collective_id=0, has_side_effects=True, vmem_limit_bytes=24000000
        ),
        name="overlap",
    )(orbitals.reshape(parts, orbs, cells), potential)
    return jnp.transpose(inter, (1, 0, 2)), applied.reshape(orbitals.shape)


def solution(mesh):
    in_specs = (P(None, ("row", "col"), "depth", None), P("depth", None))
    out_specs = (P(("row", "depth"), None, "col"), P(None, ("row", "col"), "depth", None))
    sizes = tuple(mesh.shape[axis] for axis in ("row", "col", "depth"))
    body = exchange if sizes == (4, 4, 2) else shards
    return jax.shard_map(body, mesh=mesh, in_specs=in_specs, out_specs=out_specs, check_vma=False)
```

profile of v0, /device:TPU:2, one launch (start us, length us, event | category | flops | bytes accessed | tf_op | source)
XLA Modules:
  0.0 65.6 jit_solution(17803885470047366044)
XLA Ops:
  0.6 0.0 copy-start
  0.6 1.2 %copy-done = bf16[2,64,1,4096]{3,1,2,0:T(8,128)(2,1)S(1)} copy-done((bf16[2,64,1,4096]{3,1,2,0:T(8,128)(2,1)S(1)}, bf16[2,64,1,4096]{3,1,2,0:T(8,128)(2,1)}, u32[]{:S(2)}) %copy-start) | copy-done | bytes 1048600
  1.9 0.0 copy-start.1
  1.9 0.7 %copy-done.1 = f32[1,4096]{1,0:T(1,128)S(1)} copy-done((f32[1,4096]{1,0:T(1,128)S(1)}, f32[1,4096]{1,0:T(1,128)}, u32[]{:S(2)}) %copy-start.1) | copy-done | bytes 16408
  2.6 61.1 %overlap.1 = (f32[2,128,256]{2,1,0:T(8,128)S(1)}, bf16[2,64,4096]{2,1,0:T(8,128)(2,1)S(1)}) custom-call(bf16[2,64,4096]{2,1,0:T(8,128)(2,1)S(1)} %bitcast.5, f32[1,4096]{1,0:T(1,128)S(1)} %copy-done.1), custom_call_target="tpu_custom_call" | custom-call | tf_op jit(solution)/shard_map/overlap/pallas_call | solution.py:261
  63.7 0.9 %copy.4 = f32[128,2,256]{2,1,0:T(2,128)} copy(f32[128,2,256]{2,0,1:T(8,128)S(1)} %bitcast.7) | data formatting | bytes 524288
  64.6 1.0 %copy.7 = bf16[2,64,1,4096]{3,1,2,0:T(8,128)(2,1)} copy(bf16[2,64,1,4096]{3,1,2,0:T(8,128)(2,1)S(1)} %bitcast.6) | data formatting | bytes 2097152
Async XLA Ops:
  0.6 1.2 %copy-start = (bf16[2,64,1,4096]{3,1,2,0:T(8,128)(2,1)S(1)}, bf16[2,64,1,4096]{3,1,2,0:T(8,128)(2,1)}, u32[]{:S(2)}) copy-start(bf16[2,64,1,4096]{3,1,2,0:T(8,128)(2,1)} %param.2) | copy-start | bytes 3145732
  1.9 0.7 %copy-start.1 = (f32[1,4096]{1,0:T(1,128)S(1)}, f32[1,4096]{1,0:T(1,128)}, u32[]{:S(2)}) copy-start(f32[1,4096]{1,0:T(1,128)} %pot_hbm.1) | copy-start | bytes 49156
where the time goes:
time: 65.8 us; the launch traced here: 65.6 us
  Pallas kernels  61.1 us (93%)
  local copies, waits for them, and re-layouts  3.81 us (6%)
    pallas_call x1, Pallas kernels, exchange(): pl.pallas_call(functools.partial(kernel, dvol), out_shape=(jax.ShapeDtype...  61.1 us
    unnamed x6, local copies, waits for them, and re-layouts  3.81 us

commit v1 on v0

--- a/solution.py
+++ b/solution.py
@@ -98,12 +98,39 @@
     lax.fori_loop(0, parts * (orbs // step), body, 0)
 
 
-def kernel(dvol, orb_hbm, pot_hbm, inter, applied, orb, pot, halo, panel, acc, give, take,
+STAGES = ((0, 2), (2, 3), (3, 4))
+PIECES = ((0, 0, 4), (1, 0, 5), (2, 0, 4), (2, 4, 3))
+GROUPS = 4
+OUTER, INNER = 0, 1
+MEMBERS = (
+    ((OUTER, 0), (OUTER, 1)),
+    ((OUTER, 2), (INNER, 0)),
+    ((OUTER, 3), (INNER, 1)),
+    ((INNER, 2), (INNER, 3)),
+)
+PLACE = {member: (g, u) for g, pair in enumerate(MEMBERS) for u, member in enumerate(pair)}
+
+
+def blocks():
+    order, spans = {}, []
+    for low, high in STAGES:
+        begin = len(order)
+        for a in range(high):
+            for b in range(high):
+                if max(a, b) >= low:
+                    order[a, b] = len(order)
+        spans.append((begin, len(order) - begin))
+    return order, spans
+
+
+def kernel(dvol, orb_hbm, pot_hbm, inter, applied, orb, pot, halo, panel, acc, take, pacc, ptake,
            land, relay, ins, hs, hr, ls, zs, zr, xs, xr, ds, dr, gs, gr, qr, rs, rr):
     r, c, d = lax.axis_index("row"), lax.axis_index("col"), lax.axis_index("depth")
     parts, orbs, cells = orb.shape
     quarter = cells // 4
-    half = acc.shape[2]
+    size = orbs // GROUPS
+    wide = 8 * size
+    order, spans = blocks()
     load = pltpu.make_async_copy(orb_hbm, orb, ins.at[0])
     load.start()
     load_pot = pltpu.make_async_copy(pot_hbm, pot, ins.at[1])
@@ -125,139 +152,285 @@
             device_id=dev, device_id_type=MESH,
         )
 
-    def lanes(k):
-        return pl.ds(pl.multiple_of(k * quarter, quarter), quarter)
-
-    def block(j, k, part):
-        return panel.at[j, part, pl.ds(pl.multiple_of(k * orbs, orbs), orbs), :]
-
-    zsend, xsend = {}, {}
-    for k in (1, 3, 2):
-        for p in (0, 1):
-            zsend[k, p] = send(orb.at[p, :, lanes(flip(c, k))], block(0, c, p),
-                               zs.at[k, p], zr.at[k, p], zdev[k])
-            zsend[k, p].start()
-    for p in (0, 1):
-        for j in (1, 2):
-            xsend[0, j, p] = send(orb.at[p, :, lanes(c)], block(j, c, p),
-                                  xs.at[0, j, p], xr.at[0, j, p], xdev[j])
-            xsend[0, j, p].start()
+    def own(g, k):
+        lanes = pl.ds(pl.multiple_of(k * quarter, quarter), quarter)
+        return orb.at[:, pl.ds(g * size, size), lanes]
+
+    def spot(j, m, k):
+        deep = lax.rem(k + 1, 4) >= 2
+        g, u = (jnp.where(deep, i, o) for i, o in zip(PLACE[INNER, m], PLACE[OUTER, m]))
+        return panel.at[j, g, :, u, lax.div(k, 2)]
+
+    def go(cp):
+        cp.start()
+        return cp
+
+    def flush(ref, sem):
+        pltpu.make_async_copy(ref, ref, sem).wait()
+
+    zsend, xsend, pair, cross = {}, {}, {}, {}
+    for g in range(GROUPS):
+        for k in (1, 3, 2):
+            zsend[k, g] = go(send(own(g, flip(c, k)), spot(0, g, c), zs, zr.at[k, g], zdev[k]))
+    for g in range(GROUPS):
+        for j in (1, 2):
+            xsend[0, j, g] = go(send(own(g, c), spot(j, g, c), xs, xr.at[0, j, g], xdev[j]))
     edge = send(orb, halo, hs, hr, peer)
     edge.start()
-    local = [pltpu.make_async_copy(orb.at[p, :, lanes(c)], block(0, c, p), ls.at[p])
-             for p in (0, 1)]
+    local = [pltpu.make_async_copy(own(g, c), spot(0, g, c), ls.at[g]) for g in range(GROUPS)]
     for cp in local:
         cp.start()
 
-    load_pot.wait()
-    edge.wait()
-    stencil(orb, halo, pot, applied)
-    for cp in local:
-        cp.wait()
-
-    for k in (1, 3, 2):
-        for p in (0, 1):
-            zsend[k, p].wait_recv()
-            for j in (1, 2):
-                xsend[k, j, p] = send(block(0, flip(c, k), p), block(j, flip(c, k), p),
-                                      xs.at[k, j, p], xr.at[k, j, p], xdev[j])
-                xsend[k, j, p].start()
-
-    def tile(slot, jl, jr):
-        for part in (0, 1):
-            if slot == 4 and part == 1:
-                jl, jr = jr, jl
-            a, b = panel[jl, 0], panel[jl, 1]
-            if part == 0:
-                s = contract(a, panel[jr, 0]) + contract(b, panel[jr, 1])
-            else:
-                s = contract(a, panel[jr, 1]) - contract(b, panel[jr, 0])
-            acc[slot, part] = jnp.where(d == 0, s[:half], s[half:])
-            give[slot, part] = jnp.where(d == 0, s[half:], s[:half])
-        cp = send(give.at[slot], take.at[slot], ds.at[slot], dr.at[slot], peer)
-        cp.start()
-        return cp
-
     inner = lax.rem(c + 1, 4) >= 2
-
-    def ship(t):
+    lane = lax.broadcasted_iota(jnp.int32, (1, 2 * wide // 2), 1)
+    sign = jnp.where(lane < wide // 2, 1.0, -1.0).astype(jnp.float32)
+
+    def fold(x):
+        rows = x.shape[0] // 2
+        return x[:rows] + sign * pltpu.roll(x[rows:], wide // 2, 1)
+
+    def span(s):
+        begin, count = spans[s]
+        return pl.ds(begin, count)
+
+    def forward(k, g):
+        zsend[k, g].wait_recv()
+        for j in (1, 2):
+            part = spot(0, g, flip(c, k)), spot(j, g, flip(c, k))
+            send(*part, xs, xr.at[k, j, g], xdev[j]).start()
+
+    def forwards(deep, shallow):
+        @pl.when(inner)
+        def _():
+            for k, m in deep:
+                forward(k, m)
+
+        @pl.when(jnp.logical_not(inner))
+        def _():
+            for k, m in shallow:
+                forward(k, m)
+
+    def arrived(k, m):
+        for j in (1, 2):
+            src, dst = spot(0, m, flip(c, k)), spot(j, m, flip(c, k))
+            send(src, dst, xs, xr.at[k, j, m], xdev[j]).wait_recv()
+
+    def gathered(g):
+        for kind, m in MEMBERS[g]:
+            same = inner if kind == INNER else jnp.logical_not(inner)
+
+            @pl.when(same)
+            def _():
+                arrived(0, m)
+                arrived(3, m)
+
+            @pl.when(jnp.logical_not(same))
+            def _():
+                arrived(1, m)
+                arrived(2, m)
+
+    def fresh(s):
+        return [(a, b) for a, b in order if spans[s][0] <= order[a, b] < sum(spans[s])]
+
+    def tile(t, s):
+        top = STAGES[s][1]
+        left = panel[0, 0:top].reshape(top * wide, quarter)
+        right = panel[t, 0:top].reshape(top * wide, quarter)
+        prod = contract(left, right)
+        for a, b in fresh(s):
+            x = fold(prod[a * wide:(a + 1) * wide, b * wide:(b + 1) * wide])
+            x = x.reshape(2, 2, size, wide)
+            for h in (0, 1):
+                acc[t, h, order[a, b]] = x[:, h].reshape(2 * size, wide)
+        pair[t, s] = go(send(acc.at[t, 1 - d, span(s)], take.at[t, span(s)], ds, dr.at[t, s], peer))
+
+    def shared(s):
+        top, half = STAGES[s][1], wide // 2
+        for j in (1, 2):
+            left = panel[j, 0:top, :, j - 1].reshape(top * half, quarter)
+            right = panel[3 - j, 0:top].reshape(top * wide, quarter)
+            prod = contract(left, right)
+            for a, b in fresh(s):
+                x = fold(prod[a * half:(a + 1) * half, b * wide:(b + 1) * wide])
+                for h in (0, 1):
+                    pacc[h, j - 1, order[a, b]] = x[h * size:(h + 1) * size]
+        pair[4, s] = go(send(pacc.at[1 - d, :, span(s)], ptake.at[:, span(s)], ds, dr.at[3, s], peer))
+
+    def settle(t, s):
+        pair[t, s].wait_recv()
+        acc[t, d, span(s)] += take[t, span(s)]
+
+    def swap(s):
+        pair[4, s].wait_recv()
+        pacc[d, :, span(s)] += ptake[:, span(s)]
+        for j in (1, 2):
+            dst = acc.at[3, d, span(s), pl.ds((j - 1) * size, size)]
+            cross[j, s] = go(send(pacc.at[d, j - 1, span(s)], dst, rs, rr.at[j - 1, s], xdev[j]))
+
+    def swapped(s):
+        for j in (1, 2):
+            cross[j, s].wait_recv()
+
+    def route(t):
         to = flip(r, jnp.int32(t))
         return to, lax.div(to, 2) != lax.div(c, 2)
 
-    def start_ship(t):
-        to, across = ship(t)
+    def chunk(n):
+        s, skip, count = PIECES[n]
+        return pl.ds(spans[s][0] + skip, count)
+
+    def far(t, s):
+        to, across = route(t)
+
+        @pl.when(jnp.logical_and(across, jnp.logical_not(inner)))
+        def _():
+            for n in range(len(PIECES)):
+                if PIECES[n][0] == s:
+                    send(acc.at[t, d, chunk(n)], relay.at[t, chunk(n)], gs, qr.at[t, n], zdev[1]).start()
+
+    def near(t, s):
+        to, across = route(t)
 
         @pl.when(jnp.logical_and(to != c, jnp.logical_not(across)))
         def _():
-            send(acc.at[t], land.at[0], gs.at[t], gr.at[0], zdev[1]).start()
-
-        @pl.when(jnp.logical_and(across, jnp.logical_not(inner)))
-        def _():
-            send(acc.at[t], relay.at[t], gs.at[t], qr.at[t], zdev[1]).start()
-
-    def pass_on(t):
-        to, across = ship(t)
+            send(acc.at[t, d, span(s)], land.at[0, span(s)], gs, gr.at[0, s], zdev[1]).start()
+
+    def pass_on(t, n):
+        to, across = route(t)
 
         @pl.when(jnp.logical_and(across, inner))
         def _():
-            send(acc.at[t], relay.at[t], gs.at[t], qr.at[t], zdev[1]).wait_recv()
-            acc[t] += relay[t]
-            send(acc.at[t], land.at[1], gs.at[t], gr.at[1], (r, to, d)).start()
-
-    def settle(t):
-        pair[t].wait_recv()
-        acc[t] += take[t]
-
-    pair = {0: tile(0, 0, 0)}
-    settle(0)
-    start_ship(0)
-    for k in (0, 1, 3, 2):
-        for j in (1, 2):
-            for p in (0, 1):
-                xsend[k, j, p].wait_recv()
-    pair[4] = tile(4, 1, 2)
-    pair[2] = tile(2, 0, 2)
-    settle(4)
-    cross = [send(acc.at[4, p], acc.at[3, p], rs.at[p], rr.at[p], xdev[1 + p]) for p in (0, 1)]
-    for cp in cross:
-        cp.start()
-    settle(2)
-    start_ship(2)
-    pair[1] = tile(1, 0, 1)
-    pass_on(0)
-    settle(1)
-    for cp in cross:
-        cp.wait_recv()
-    start_ship(3)
-    start_ship(1)
-    pass_on(2)
-    pass_on(3)
-    pass_on(1)
-
-    total = acc[flip(r, c)]
-    for k in (0, 1):
-        send(acc.at[0], land.at[k], gs.at[0], gr.at[k], zdev[1]).wait_recv()
-        total = total + land[k]
-    inter[...] = total * dvol
-
-    for cp in [edge] + cross + list(pair.values()) + list(zsend.values()) + list(xsend.values()):
-        if cp is not edge:
-            cp.wait_send()
-    for t in (0, 1, 2, 3):
-        to, across = ship(t)
-
-        @pl.when(to != c)
-        def _():
-            send(acc.at[t], land.at[0], gs.at[t], gr.at[0], zdev[1]).wait_send()
+            send(acc.at[t, d, chunk(n)], relay.at[t, chunk(n)], gs, qr.at[t, n], zdev[1]).wait_recv()
+            acc[t, d, chunk(n)] += relay[t, chunk(n)]
+            send(acc.at[t, d, chunk(n)], land.at[1, chunk(n)], gs, gr.at[1, n], (r, to, d)).start()
+
+    def operator():
+        load_pot.wait()
+        edge.wait()
+        stencil(orb, halo, pot, applied)
+        for cp in local:
+            cp.wait()
+
+    operator()
+    forwards(((1, 0), (3, 0), (2, 0), (1, 1), (2, 1), (1, 2), (2, 2)), ((1, 0), (3, 0), (2, 0), (3, 1), (1, 1), (3, 2)))
+    tile(0, 0)
+    forwards(((1, 3), (2, 3)), ((1, 2), (1, 3)))
+    settle(0, 0)
+    far(0, 0)
+    near(0, 0)
+    gathered(0)
+    gathered(1)
+    shared(0)
+    forwards((), ((3, 3),))
+    tile(2, 0)
+    forwards(((3, 1),), ((2, 1),))
+    tile(1, 0)
+    swap(0)
+    settle(2, 0)
+    far(2, 0)
+    settle(1, 0)
+    far(1, 0)
+    near(2, 0)
+    near(1, 0)
+    tile(0, 1)
+    forwards(((3, 2),), ((2, 2),))
+    settle(0, 1)
+    far(0, 1)
+    near(0, 1)
+    gathered(2)
+    shared(1)
+    forwards(((3, 3),), ((2, 3),))
+    tile(2, 1)
+    tile(1, 1)
+    swapped(0)
+    far(3, 0)
+    near(3, 0)
+    tile(0, 2)
+    swap(1)
+    settle(2, 1)
+    far(2, 1)
+    settle(1, 1)
+    far(1, 1)
+    near(2, 1)
+    near(1, 1)
+    for t in (0, 2, 1, 3):
+        pass_on(t, 0)
+    pass_on(0, 1)
+    gathered(3)
+    shared(2)
+    tile(2, 2)
+    tile(1, 2)
+    settle(0, 2)
+    far(0, 2)
+    swapped(1)
+    far(3, 1)
+    near(3, 1)
+    swap(2)
+    settle(2, 2)
+    far(2, 2)
+    settle(1, 2)
+    far(1, 2)
+    near(2, 2)
+    for t in (2, 1, 3):
+        pass_on(t, 1)
+    pass_on(0, 2)
+    pass_on(0, 3)
+    swapped(2)
+    far(3, 2)
+    near(3, 2)
+    near(0, 2)
+    near(1, 2)
+    pass_on(2, 2)
+    pass_on(1, 2)
+    pass_on(2, 3)
+    pass_on(1, 3)
+    pass_on(3, 2)
+    pass_on(3, 3)
+
+    flush(panel.at[0, 0:3], zs)
+    flush(panel.at[0:2], xs)
+    flush(acc.at[0:2], ds)
+    flush(acc.at[0, 0], rs)
+    mine = flip(r, c)
+    for s in range(len(STAGES)):
+        send(acc.at[0, d, span(s)], land.at[0, span(s)], gs, gr.at[0, s], zdev[1]).wait_recv()
+    for n in range(len(PIECES)):
+        send(acc.at[0, d, chunk(n)], land.at[1, chunk(n)], gs, gr.at[1, n], zdev[1]).wait_recv()
+    half, quad = wide // 2, wide // 8
+    pick = lax.div(lane, quad)
+    for a in range(GROUPS):
+        for u, (kind, m) in enumerate(MEMBERS[a]):
+            total = []
+            for b in range(GROUPS):
+                i, rows = order[a, b], pl.ds(u * size, size)
+                total.append((acc[mine, d, i, rows] + land[0, i, rows] + land[1, i, rows]) * dvol)
+            first = (d if kind == OUTER else 1 - d) * half + m * size
+            for part in range(parts):
+                for v in (0, 1):
+                    out = None
+                    for b in range(GROUPS):
+                        for w, (col, n) in enumerate(MEMBERS[b]):
+                            at = part * half + w * 2 * quad + v * quad
+                            to = (col ^ v) * half + n * quad
+                            moved = pltpu.roll(total[b], (to - at) % wide, 1)
+                            out = moved if out is None else jnp.where(pick == to // quad, moved, out)
+                    rows = pl.ds(pl.multiple_of(first, size), size)
+                    inter[part, rows, pl.ds(v * wide, wide)] = out
+
+    flush(relay.at[0:3], gs)
 
 
 def exchange(orbitals, potential):
     parts, orbs, planes, cells = orbitals.shape
     rows = orbs * lax.axis_size("col")
     half = rows // 2
+    size = orbs // GROUPS
+    count = GROUPS * GROUPS
+    steps, pieces = len(STAGES), len(PIECES)
     dvol = 1.0 / (planes * lax.axis_size("depth") * cells)
     vmem = pl.BlockSpec(memory_space=pltpu.VMEM)
     dma = pltpu.SemaphoreType.DMA
+    block = (count, 2 * size, 8 * size)
     inter, applied = pl.pallas_call(
         functools.partial(kernel, dvol),
         out_shape=(
@@ -270,17 +443,19 @@
             pltpu.VMEM((parts, orbs, cells), jnp.bfloat16),
             pltpu.VMEM(potential.shape, jnp.float32),
             pltpu.VMEM((parts, orbs, cells), jnp.bfloat16),
-            pltpu.VMEM((3, parts, rows, cells // 4), jnp.bfloat16),
-            pltpu.VMEM((5, 2, half, rows), jnp.float32),
-            pltpu.VMEM((5, 2, half, rows), jnp.float32),
-            pltpu.VMEM((5, 2, half, rows), jnp.float32),
-            pltpu.VMEM((2, 2, half, rows), jnp.float32),
-            pltpu.VMEM((4, 2, half, rows), jnp.float32),
-            dma((2,)), dma, dma, dma((2,)), dma((4, 2)), dma((4, 2)), dma((4, 3, 2)),
-            dma((4, 3, 2)), dma((5,)), dma((5,)), dma((4,)), dma((2,)), dma((4,)), dma((2,)), dma((2,)),
+            pltpu.VMEM((3, GROUPS, parts, 2, 2, size, cells // 4), jnp.bfloat16),
+            pltpu.VMEM((4, 2) + block, jnp.float32),
+            pltpu.VMEM((3,) + block, jnp.float32),
+            pltpu.VMEM((2, 2, count, size, 8 * size), jnp.float32),
+            pltpu.VMEM((2, count, size, 8 * size), jnp.float32),
+            pltpu.VMEM((2,) + block, jnp.float32),
+            pltpu.VMEM((4,) + block, jnp.float32),
+            dma((2,)), dma, dma, dma((GROUPS,)), dma, dma((4, GROUPS)), dma,
+            dma((4, 3, GROUPS)), dma, dma((4, steps)), dma, dma((2, pieces)),
+            dma((4, pieces)), dma, dma((2, steps)),
         ],
         compiler_params=pltpu.CompilerParams(
-            collective_id=0, has_side_effects=True, vmem_limit_bytes=24000000
+            collective_id=0, has_side_effects=True, vmem_limit_bytes=55000000
         ),
         name="overlap",
     )(orbitals.reshape(parts, orbs, cells), potential)

time: 65.8 us -> 51.8 us (0.79)
  the two profiles are of different devices: /device:TPU:2 before, /device:TPU:6 now
where the time goes in v1:
time: 51.8 us; the launch traced here: 51.6 us
  Pallas kernels  48.4 us (93%)
  local copies, waits for them, and re-layouts  2.59 us (5%)
  between operations  0.65 us (1%)
    pallas_call x1, Pallas kernels, exchange(): pl.pallas_call(functools.partial(kernel, dvol), out_shape=(jax.ShapeDtype...  48.4 us
    unnamed x4, local copies, waits for them, and re-layouts  2.59 us

profile of v1, /device:TPU:6, one launch (start us, length us, event | category | flops | bytes accessed | tf_op | source)
XLA Modules:
  0.0 51.6 jit_solution(5311806647659551672)
XLA Ops:
  0.6 0.0 copy-start
  0.6 0.7 %copy-done = f32[1,4096]{1,0:T(1,128)S(1)} copy-done((f32[1,4096]{1,0:T(1,128)S(1)}, f32[1,4096]{1,0:T(1,128)}, u32[]{:S(2)}) %copy-start) | copy-done | bytes 16408
  1.3 48.4 %overlap.1 = (f32[2,128,256]{2,1,0:T(8,128)S(1)}, bf16[2,64,4096]{2,1,0:T(8,128)(2,1)S(1)}) custom-call(bf16[2,64,4096]{2,1,0:T(8,128)(2,1)} %bitcast.7, f32[1,4096]{1,0:T(1,128)S(1)} %copy-done), custom_call_target="tpu_custom_call" | custom-call | tf_op jit(solution)/shard_map/overlap/pallas_call | solution.py:434
  49.7 0.9 %copy.4 = f32[128,2,256]{2,1,0:T(2,128)} copy(f32[128,2,256]{2,0,1:T(8,128)S(1)} %bitcast.6) | data formatting | bytes 524288
  50.6 1.0 %copy.7 = bf16[2,64,1,4096]{3,1,2,0:T(8,128)(2,1)} copy(bf16[2,64,1,4096]{3,1,2,0:T(8,128)(2,1)S(1)} %bitcast.5) | data formatting | bytes 2097152
Async XLA Ops:
  0.6 0.7 %copy-start = (f32[1,4096]{1,0:T(1,128)S(1)}, f32[1,4096]{1,0:T(1,128)}, u32[]{:S(2)}) copy-start(f32[1,4096]{1,0:T(1,128)} %pot_hbm.1) | copy-start | bytes 49156

commit v2 on v1

--- a/solution.py
+++ b/solution.py
@@ -123,8 +123,8 @@
     return order, spans
 
 
-def kernel(dvol, orb_hbm, pot_hbm, inter, applied, orb, pot, halo, panel, acc, take, pacc, ptake,
-           land, relay, ins, hs, hr, ls, zs, zr, xs, xr, ds, dr, gs, gr, qr, rs, rr):
+def kernel(dvol, orb_hbm, pot_hbm, inter, applied, orb, pot, halo, panel, acc, take, pacc, cross,
+           land, relay, ptake, wire, ins, hs, hr, ls, zs, zr, xs, xr, ds, dr, gs, gr, qr, rs, rr, ps, pr, fs, fr):
     r, c, d = lax.axis_index("row"), lax.axis_index("col"), lax.axis_index("depth")
     parts, orbs, cells = orb.shape
     quarter = cells // 4
@@ -140,7 +140,7 @@
     xdev = [None] + [(flip(r, k), c, d) for k in (1, 2)]
 
     barrier = pltpu.get_barrier_semaphore()
-    friends = [peer] + zdev[1:] + xdev[1:]
+    friends = [peer] + zdev[1:] + xdev[1:] + [(flip(r, k), c, 1 - d) for k in (1, 2)]
     for dev in friends:
         pl.semaphore_signal(barrier, inc=1, device_id=dev, device_id_type=MESH)
     load.wait()
@@ -156,9 +156,15 @@
         lanes = pl.ds(pl.multiple_of(k * quarter, quarter), quarter)
         return orb.at[:, pl.ds(g * size, size), lanes]
 
+    def place(m, k):
+        deep = lax.rem(k + 1, 4) >= 2
+        return [jnp.where(deep, i, o) for i, o in zip(PLACE[INNER, m], PLACE[OUTER, m])]
+
+    def home(m, k):
+        return place(m, k)[0]
+
     def spot(j, m, k):
-        deep = lax.rem(k + 1, 4) >= 2
-        g, u = (jnp.where(deep, i, o) for i, o in zip(PLACE[INNER, m], PLACE[OUTER, m]))
+        g, u = place(m, k)
         return panel.at[j, g, :, u, lax.div(k, 2)]
 
     def go(cp):
@@ -168,18 +174,17 @@
     def flush(ref, sem):
         pltpu.make_async_copy(ref, ref, sem).wait()
 
-    zsend, xsend, pair, cross = {}, {}, {}, {}
+    zsend, pair = {}, {}
     for g in range(GROUPS):
         for k in (1, 3, 2):
             zsend[k, g] = go(send(own(g, flip(c, k)), spot(0, g, c), zs, zr.at[k, g], zdev[k]))
     for g in range(GROUPS):
         for j in (1, 2):
-            xsend[0, j, g] = go(send(own(g, c), spot(j, g, c), xs, xr.at[0, j, g], xdev[j]))
+            send(own(g, c), spot(j, g, c), xs, xr.at[home(g, c)], xdev[j]).start()
     edge = send(orb, halo, hs, hr, peer)
     edge.start()
-    local = [pltpu.make_async_copy(own(g, c), spot(0, g, c), ls.at[g]) for g in range(GROUPS)]
-    for cp in local:
-        cp.start()
+    for g in range(GROUPS):
+        pltpu.make_async_copy(own(g, c), spot(0, g, c), ls).start()
 
     inner = lax.rem(c + 1, 4) >= 2
     lane = lax.broadcasted_iota(jnp.int32, (1, 2 * wide // 2), 1)
@@ -197,7 +202,7 @@
         zsend[k, g].wait_recv()
         for j in (1, 2):
             part = spot(0, g, flip(c, k)), spot(j, g, flip(c, k))
-            send(*part, xs, xr.at[k, j, g], xdev[j]).start()
+            send(*part, xs, xr.at[home(g, flip(c, k))], xdev[j]).start()
 
     def forwards(deep, shallow):
         @pl.when(inner)
@@ -210,24 +215,10 @@
             for k, m in shallow:
                 forward(k, m)
 
-    def arrived(k, m):
-        for j in (1, 2):
-            src, dst = spot(0, m, flip(c, k)), spot(j, m, flip(c, k))
-            send(src, dst, xs, xr.at[k, j, m], xdev[j]).wait_recv()
+    last = len(STAGES) - 1
 
     def gathered(g):
-        for kind, m in MEMBERS[g]:
-            same = inner if kind == INNER else jnp.logical_not(inner)
-
-            @pl.when(same)
-            def _():
-                arrived(0, m)
-                arrived(3, m)
-
-            @pl.when(jnp.logical_not(same))
-            def _():
-                arrived(1, m)
-                arrived(2, m)
+        flush(panel.at[1:3, g], xr.at[g])
 
     def fresh(s):
         return [(a, b) for a, b in order if spans[s][0] <= order[a, b] < sum(spans[s])]
@@ -254,22 +245,47 @@
                 x = fold(prod[a * half:(a + 1) * half, b * wide:(b + 1) * wide])
                 for h in (0, 1):
                     pacc[h, j - 1, order[a, b]] = x[h * size:(h + 1) * size]
-        pair[4, s] = go(send(pacc.at[1 - d, :, span(s)], ptake.at[:, span(s)], ds, dr.at[3, s], peer))
+            if s == last:
+                for h in (0, 1):
+                    dev = (flip(r, jnp.int32(j)), c, jnp.int32(h))
+                    send(pacc.at[h, j - 1, span(s)], cross.at[j - 1, d], fs, fr, dev).start()
+        if s < last:
+            send(pacc.at[1 - d, :, span(s)], ptake.at[:, span(s)], ps, pr.at[s], peer).start()
 
     def settle(t, s):
         pair[t, s].wait_recv()
         acc[t, d, span(s)] += take[t, span(s)]
 
     def swap(s):
-        pair[4, s].wait_recv()
+        flush(ptake.at[:, span(s)], pr.at[s])
         pacc[d, :, span(s)] += ptake[:, span(s)]
         for j in (1, 2):
             dst = acc.at[3, d, span(s), pl.ds((j - 1) * size, size)]
-            cross[j, s] = go(send(pacc.at[d, j - 1, span(s)], dst, rs, rr.at[j - 1, s], xdev[j]))
+            send(pacc.at[d, j - 1, span(s)], dst, rs, rr.at[s], xdev[j]).start()
 
     def swapped(s):
-        for j in (1, 2):
-            cross[j, s].wait_recv()
+        if s < last:
+            flush(acc.at[3, d, span(s)], rr.at[s])
+        else:
+            flush(cross, fr)
+            for j in (0, 1):
+                acc[3, d, span(s), pl.ds(j * size, size)] = cross[j, 0] + cross[j, 1]
+
+    def encode(t, blocks):
+        x = acc[t, d, blocks]
+        high = x.astype(jnp.bfloat16)
+        base = high.astype(jnp.float32)
+        steps = jnp.round((x - base) / jnp.maximum(jnp.abs(base), 1e-37) * 2048.0)
+        steps = jnp.clip(steps, -7.0, 7.0)
+        wire[t, blocks, :2 * size] = high
+        wire[t, blocks, 2 * size:] = (steps[:, :size] * 16.0 + steps[:, size:]).astype(jnp.bfloat16)
+
+    def decode(words):
+        base = words[:, :2 * size].astype(jnp.float32)
+        code = words[:, 2 * size:].astype(jnp.float32)
+        first = jnp.round(code / 16.0)
+        steps = jnp.concatenate([first, code - 16.0 * first], axis=1)
+        return base + steps * jnp.abs(base) / 2048.0
 
     def route(t):
         to = flip(r, jnp.int32(t))
@@ -286,30 +302,34 @@
         def _():
             for n in range(len(PIECES)):
                 if PIECES[n][0] == s:
-                    send(acc.at[t, d, chunk(n)], relay.at[t, chunk(n)], gs, qr.at[t, n], zdev[1]).start()
-
-    def near(t, s):
+                    encode(t, chunk(n))
+                    send(wire.at[t, chunk(n)], relay.at[t, chunk(n)], gs, qr.at[t, n], zdev[1]).start()
+
+    def near(t, s, side):
         to, across = route(t)
 
-        @pl.when(jnp.logical_and(to != c, jnp.logical_not(across)))
+        @pl.when(jnp.logical_and(jnp.logical_and(to != c, jnp.logical_not(across)), side))
         def _():
-            send(acc.at[t, d, span(s)], land.at[0, span(s)], gs, gr.at[0, s], zdev[1]).start()
+            encode(t, span(s))
+            send(wire.at[t, span(s)], land.at[0, span(s)], gs, gr, zdev[1]).start()
 
     def pass_on(t, n):
         to, across = route(t)
 
         @pl.when(jnp.logical_and(across, inner))
         def _():
-            send(acc.at[t, d, chunk(n)], relay.at[t, chunk(n)], gs, qr.at[t, n], zdev[1]).wait_recv()
-            acc[t, d, chunk(n)] += relay[t, chunk(n)]
-            send(acc.at[t, d, chunk(n)], land.at[1, chunk(n)], gs, gr.at[1, n], (r, to, d)).start()
+            flush(relay.at[t, chunk(n)], qr.at[t, n])
+            acc[t, d, chunk(n)] += decode(relay[t, chunk(n)])
+            encode(t, chunk(n))
+            send(wire.at[t, chunk(n)], land.at[1, chunk(n)], gs, gr, (r, to, d)).start()
+
+    deep, edge_chip = inner, jnp.logical_not(inner)
 
     def operator():
         load_pot.wait()
         edge.wait()
         stencil(orb, halo, pot, applied)
-        for cp in local:
-            cp.wait()
+        flush(panel.at[0, 0], ls)
 
     operator()
     forwards(((1, 0), (3, 0), (2, 0), (1, 1), (2, 1), (1, 2), (2, 2)), ((1, 0), (3, 0), (2, 0), (3, 1), (1, 1), (3, 2)))
@@ -317,7 +337,7 @@
     forwards(((1, 3), (2, 3)), ((1, 2), (1, 3)))
     settle(0, 0)
     far(0, 0)
-    near(0, 0)
+    near(0, 0, True)
     gathered(0)
     gathered(1)
     shared(0)
@@ -330,56 +350,62 @@
     far(2, 0)
     settle(1, 0)
     far(1, 0)
-    near(2, 0)
-    near(1, 0)
+    near(2, 0, True)
+    near(1, 0, True)
     tile(0, 1)
     forwards(((3, 2),), ((2, 2),))
     settle(0, 1)
     far(0, 1)
-    near(0, 1)
-    gathered(2)
-    shared(1)
-    forwards(((3, 3),), ((2, 3),))
-    tile(2, 1)
-    tile(1, 1)
+    near(0, 1, True)
     swapped(0)
     far(3, 0)
-    near(3, 0)
-    tile(0, 2)
+    near(3, 0, True)
+    gathered(2)
+    forwards(((3, 3),), ((2, 3),))
+    shared(1)
+    pass_on(0, 0)
+    pass_on(2, 0)
+    tile(2, 1)
+    pass_on(1, 0)
+    tile(1, 1)
     swap(1)
     settle(2, 1)
     far(2, 1)
+    pass_on(0, 1)
+    tile(0, 2)
     settle(1, 1)
     far(1, 1)
-    near(2, 1)
-    near(1, 1)
-    for t in (0, 2, 1, 3):
-        pass_on(t, 0)
-    pass_on(0, 1)
+    near(2, 1, True)
+    near(1, 1, True)
+    pass_on(3, 0)
     gathered(3)
     shared(2)
     tile(2, 2)
-    tile(1, 2)
     settle(0, 2)
     far(0, 2)
+    near(0, 2, deep)
     swapped(1)
     far(3, 1)
-    near(3, 1)
-    swap(2)
+    near(3, 1, deep)
+    pass_on(2, 1)
+    tile(1, 2)
+    pass_on(1, 1)
     settle(2, 2)
     far(2, 2)
+    near(2, 2, deep)
     settle(1, 2)
     far(1, 2)
-    near(2, 2)
-    for t in (2, 1, 3):
-        pass_on(t, 1)
+    near(1, 2, deep)
+    near(3, 1, edge_chip)
+    near(2, 2, edge_chip)
     pass_on(0, 2)
     pass_on(0, 3)
     swapped(2)
     far(3, 2)
-    near(3, 2)
-    near(0, 2)
-    near(1, 2)
+    near(3, 2, True)
+    near(0, 2, edge_chip)
+    near(1, 2, edge_chip)
+    pass_on(3, 1)
     pass_on(2, 2)
     pass_on(1, 2)
     pass_on(2, 3)
@@ -389,13 +415,13 @@
 
     flush(panel.at[0, 0:3], zs)
     flush(panel.at[0:2], xs)
-    flush(acc.at[0:2], ds)
-    flush(acc.at[0, 0], rs)
+    flush(take, ds)
+    flush(acc.at[3, 0, 0:spans[last][0]], rs)
+    flush(ptake, ps)
+    flush(cross, fs)
     mine = flip(r, c)
-    for s in range(len(STAGES)):
-        send(acc.at[0, d, span(s)], land.at[0, span(s)], gs, gr.at[0, s], zdev[1]).wait_recv()
-    for n in range(len(PIECES)):
-        send(acc.at[0, d, chunk(n)], land.at[1, chunk(n)], gs, gr.at[1, n], zdev[1]).wait_recv()
+    flush(land, gr)
+    acc[mine, d] = (acc[mine, d] + decode(land[0]) + decode(land[1])) * dvol
     half, quad = wide // 2, wide // 8
     pick = lax.div(lane, quad)
     for a in range(GROUPS):
@@ -403,7 +429,7 @@
             total = []
             for b in range(GROUPS):
                 i, rows = order[a, b], pl.ds(u * size, size)
-                total.append((acc[mine, d, i, rows] + land[0, i, rows] + land[1, i, rows]) * dvol)
+                total.append(acc[mine, d, i, rows])
             first = (d if kind == OUTER else 1 - d) * half + m * size
             for part in range(parts):
                 for v in (0, 1):
@@ -420,6 +446,21 @@
     flush(relay.at[0:3], gs)
 
 
+def publish(inter, applied, inter_out, applied_out, mixed, sems):
+    whole = pltpu.make_async_copy(applied, applied_out, sems.at[0])
+    whole.start()
+    for part in (0, 1):
+        mixed[:, part, :] = inter[part]
+    tiles = pltpu.make_async_copy(mixed, inter_out, sems.at[1])
+    tiles.start()
+    whole.wait()
+    tiles.wait()
+
+
+def stay(array):
+    return pltpu.with_memory_space_constraint(array, pltpu.HBM)
+
+
 def exchange(orbitals, potential):
     parts, orbs, planes, cells = orbitals.shape
     rows = orbs * lax.axis_size("col")
@@ -431,6 +472,7 @@
     vmem = pl.BlockSpec(memory_space=pltpu.VMEM)
     dma = pltpu.SemaphoreType.DMA
     block = (count, 2 * size, 8 * size)
+    early = blocks()[1][-1][0]
     inter, applied = pl.pallas_call(
         functools.partial(kernel, dvol),
         out_shape=(
@@ -447,19 +489,32 @@
             pltpu.VMEM((4, 2) + block, jnp.float32),
             pltpu.VMEM((3,) + block, jnp.float32),
             pltpu.VMEM((2, 2, count, size, 8 * size), jnp.float32),
-            pltpu.VMEM((2, count, size, 8 * size), jnp.float32),
-            pltpu.VMEM((2,) + block, jnp.float32),
-            pltpu.VMEM((4,) + block, jnp.float32),
-            dma((2,)), dma, dma, dma((GROUPS,)), dma, dma((4, GROUPS)), dma,
-            dma((4, 3, GROUPS)), dma, dma((4, steps)), dma, dma((2, pieces)),
-            dma((4, pieces)), dma, dma((2, steps)),
+            pltpu.VMEM((2, 2, count - early, size, 8 * size), jnp.float32),
+            pltpu.VMEM((2, count, 3 * size, 8 * size), jnp.bfloat16),
+            pltpu.VMEM((4, count, 3 * size, 8 * size), jnp.bfloat16),
+            pltpu.VMEM((2, early, size, 8 * size), jnp.float32),
+            pltpu.VMEM((4, count, 3 * size, 8 * size), jnp.bfloat16),
+            dma((2,)), dma, dma, dma, dma, dma((4, GROUPS)), dma, dma((GROUPS,)), dma, dma((3, steps)),
+            dma, dma, dma((4, pieces)), dma, dma((steps,)), dma, dma((steps,)), dma, dma,
         ],
         compiler_params=pltpu.CompilerParams(
-            collective_id=0, has_side_effects=True, vmem_limit_bytes=55000000
+            collective_id=0, has_side_effects=True, vmem_limit_bytes=24000000
         ),
         name="overlap",
-    )(orbitals.reshape(parts, orbs, cells), potential)
-    return jnp.transpose(inter, (1, 0, 2)), applied.reshape(orbitals.shape)
+    )(stay(orbitals.reshape(parts, orbs, cells)), stay(potential))
+    inter, applied = pl.pallas_call(
+        publish,
+        out_shape=(
+            jax.ShapeDtypeStruct((half, 2, rows), jnp.float32),
+            jax.ShapeDtypeStruct((parts, orbs, cells), jnp.bfloat16),
+        ),
+        in_specs=[vmem, vmem],
+        out_specs=[pl.BlockSpec(memory_space=pltpu.HBM)] * 2,
+        scratch_shapes=[pltpu.VMEM((half, 2, rows), jnp.float32), dma((2,))],
+        compiler_params=pltpu.CompilerParams(vmem_limit_bytes=16000000),
+        name="publish",
+    )(inter, applied)
+    return inter, applied.reshape(orbitals.shape)
 
 
 def solution(mesh):

time: 51.8 us -> 47.8 us (0.923)
  local copies, waits for them, and re-layouts: 2.59 us -> 0 us
  Pallas kernels: 48.4 us -> 46.7 us
    pallas_call x1, Pallas kernels: 48.4 us -> 45.6 us  [exchange(): pl.pallas_call(functools.partial(kernel, dvol), out_shape=(jax.ShapeDtype...]
    unnamed x4 -> x0, local copies, waits for them, and re-layouts: 2.59 us -> none
    pallas_call x0 -> x1, Pallas kernels: none -> 1.07 us  [exchange(): pl.pallas_call(publish, out_shape=(jax.ShapeDtypeStruct((half, 2, rows),...]
where the time goes in v2:
time: 47.8 us; the launch traced here: 47.3 us
  Pallas kernels  46.7 us (98%)
  between operations  0.64 us (1%)
    pallas_call x1, Pallas kernels, exchange(): pl.pallas_call(functools.partial(kernel, dvol), out_shape=(jax.ShapeDtype...  45.6 us
    pallas_call x1, Pallas kernels, exchange(): pl.pallas_call(publish, out_shape=(jax.ShapeDtypeStruct((half, 2, rows),...  1.07 us

profile of v2, /device:TPU:6, one launch (start us, length us, event | category | flops | bytes accessed | tf_op | source)
XLA Modules:
  0.0 47.3 jit_solution(2022528097957456135)
XLA Ops:
  0.6 45.6 %overlap.1 = (f32[2,128,256]{2,1,0:T(8,128)S(1)}, bf16[2,64,4096]{2,1,0:T(8,128)(2,1)S(1)}) custom-call(bf16[2,64,4096]{2,1,0:T(8,128)(2,1)} %bitcast.4, f32[1,4096]{1,0:T(1,128)} %pot_hbm.1), custom_call_target="tpu_custom_call" | custom-call | tf_op jit(solution)/shard_map/overlap/pallas_call | solution.py:476
  46.3 1.1 %publish.1 = (f32[128,2,256]{2,1,0:T(2,128)}, bf16[2,64,4096]{2,1,0:T(8,128)(2,1)}) custom-call(f32[2,128,256]{2,1,0:T(8,128)S(1)} %get-tuple-element.6.inter, bf16[2,64,4096]{2,1,0:T(8,128)(2,1)S(1)} %get-tuple-element.7.applied), custom_call_target="tpu_custom_call" | custom-call | tf_op jit(solution)/shard_map/publish/pallas_call | solution.py:505

commit v3 on v2

--- a/solution.py
+++ b/solution.py
@@ -108,6 +108,7 @@
     ((OUTER, 3), (INNER, 1)),
     ((INNER, 2), (INNER, 3)),
 )
+CUTS = ((0, 0, 2), (1, 0, 2), (2, 0, 2), (3, 0, 1), (3, 1, 1))
 PLACE = {member: (g, u) for g, pair in enumerate(MEMBERS) for u, member in enumerate(pair)}
 
 
@@ -124,7 +125,7 @@
 
 
 def kernel(dvol, orb_hbm, pot_hbm, inter, applied, orb, pot, halo, panel, acc, take, pacc, cross,
-           land, relay, ptake, wire, ins, hs, hr, ls, zs, zr, xs, xr, ds, dr, gs, gr, qr, rs, rr, ps, pr, fs, fr):
+           land, relay, ptake, ins, hs, hr, ls, zs, zr, xs, xr, ds, dr, gs, gr, qr, rs, rr, ps, pr, fs, fr):
     r, c, d = lax.axis_index("row"), lax.axis_index("col"), lax.axis_index("depth")
     parts, orbs, cells = orb.shape
     quarter = cells // 4
@@ -152,9 +153,10 @@
             device_id=dev, device_id_type=MESH,
         )
 
-    def own(g, k):
-        lanes = pl.ds(pl.multiple_of(k * quarter, quarter), quarter)
-        return orb.at[:, pl.ds(g * size, size), lanes]
+    def own(m, k, begin=0, count=2):
+        half = quarter // 2
+        lanes = pl.ds(pl.multiple_of(k * quarter + begin * half, half), count * half)
+        return orb.at[:, pl.ds(m * size, size), lanes]
 
     def place(m, k):
         deep = lax.rem(k + 1, 4) >= 2
@@ -163,9 +165,10 @@
     def home(m, k):
         return place(m, k)[0]
 
-    def spot(j, m, k):
+    def spot(j, m, k, begin=0, count=2):
         g, u = place(m, k)
-        return panel.at[j, g, :, u, lax.div(k, 2)]
+        half = quarter // 2
+        return panel.at[j, g, :, u, lax.div(k, 2), :, pl.ds(begin * half, count * half)]
 
     def go(cp):
         cp.start()
@@ -174,10 +177,10 @@
     def flush(ref, sem):
         pltpu.make_async_copy(ref, ref, sem).wait()
 
-    zsend, pair = {}, {}
-    for g in range(GROUPS):
+    zsend = {}
+    for n, (m, *cut) in enumerate(CUTS):
         for k in (1, 3, 2):
-            zsend[k, g] = go(send(own(g, flip(c, k)), spot(0, g, c), zs, zr.at[k, g], zdev[k]))
+            zsend[k, n] = go(send(own(m, flip(c, k), *cut), spot(0, m, c, *cut), zs, zr.at[k, n], zdev[k]))
     for g in range(GROUPS):
         for j in (1, 2):
             send(own(g, c), spot(j, g, c), xs, xr.at[home(g, c)], xdev[j]).start()
@@ -198,11 +201,12 @@
         begin, count = spans[s]
         return pl.ds(begin, count)
 
-    def forward(k, g):
-        zsend[k, g].wait_recv()
+    def forward(k, n):
+        zsend[k, n].wait_recv()
+        m, *cut = CUTS[n]
         for j in (1, 2):
-            part = spot(0, g, flip(c, k)), spot(j, g, flip(c, k))
-            send(*part, xs, xr.at[home(g, flip(c, k))], xdev[j]).start()
+            part = [spot(i, m, flip(c, k), *cut) for i in (0, j)]
+            send(*part, xs, xr.at[home(m, flip(c, k))], xdev[j]).start()
 
     def forwards(deep, shallow):
         @pl.when(inner)
@@ -233,7 +237,7 @@
             x = x.reshape(2, 2, size, wide)
             for h in (0, 1):
                 acc[t, h, order[a, b]] = x[:, h].reshape(2 * size, wide)
-        pair[t, s] = go(send(acc.at[t, 1 - d, span(s)], take.at[t, span(s)], ds, dr.at[t, s], peer))
+        send(acc.at[t, 1 - d, span(s)], take.at[t, span(s)], ds, dr.at[t, s], peer).start()
 
     def shared(s):
         top, half = STAGES[s][1], wide // 2
@@ -253,7 +257,7 @@
             send(pacc.at[1 - d, :, span(s)], ptake.at[:, span(s)], ps, pr.at[s], peer).start()
 
     def settle(t, s):
-        pair[t, s].wait_recv()
+        flush(take.at[t, span(s)], dr.at[t, s])
         acc[t, d, span(s)] += take[t, span(s)]
 
     def swap(s):
@@ -271,59 +275,42 @@
             for j in (0, 1):
                 acc[3, d, span(s), pl.ds(j * size, size)] = cross[j, 0] + cross[j, 1]
 
-    def encode(t, blocks):
-        x = acc[t, d, blocks]
-        high = x.astype(jnp.bfloat16)
-        base = high.astype(jnp.float32)
-        steps = jnp.round((x - base) / jnp.maximum(jnp.abs(base), 1e-37) * 2048.0)
-        steps = jnp.clip(steps, -7.0, 7.0)
-        wire[t, blocks, :2 * size] = high
-        wire[t, blocks, 2 * size:] = (steps[:, :size] * 16.0 + steps[:, size:]).astype(jnp.bfloat16)
-
-    def decode(words):
-        base = words[:, :2 * size].astype(jnp.float32)
-        code = words[:, 2 * size:].astype(jnp.float32)
-        first = jnp.round(code / 16.0)
-        steps = jnp.concatenate([first, code - 16.0 * first], axis=1)
-        return base + steps * jnp.abs(base) / 2048.0
-
     def route(t):
-        to = flip(r, jnp.int32(t))
+        to = flip(r, jnp.asarray(t, jnp.int32))
         return to, lax.div(to, 2) != lax.div(c, 2)
 
     def chunk(n):
         s, skip, count = PIECES[n]
         return pl.ds(spans[s][0] + skip, count)
 
-    def far(t, s):
+    def far(t, s, side=True):
         to, across = route(t)
 
-        @pl.when(jnp.logical_and(across, jnp.logical_not(inner)))
+        @pl.when(jnp.logical_and(jnp.logical_and(across, jnp.logical_not(inner)), side))
         def _():
             for n in range(len(PIECES)):
                 if PIECES[n][0] == s:
-                    encode(t, chunk(n))
-                    send(wire.at[t, chunk(n)], relay.at[t, chunk(n)], gs, qr.at[t, n], zdev[1]).start()
-
-    def near(t, s, side):
+                    send(acc.at[t, d, chunk(n)], relay.at[t, chunk(n)], gs, qr.at[t, n], zdev[1]).start()
+
+    def near(t, s, side=True):
         to, across = route(t)
 
         @pl.when(jnp.logical_and(jnp.logical_and(to != c, jnp.logical_not(across)), side))
         def _():
-            encode(t, span(s))
-            send(wire.at[t, span(s)], land.at[0, span(s)], gs, gr, zdev[1]).start()
-
-    def pass_on(t, n):
+            send(acc.at[t, d, span(s)], land.at[0, span(s)], gs, gr, zdev[1]).start()
+
+    def pass_on(t, n, side=True):
         to, across = route(t)
 
-        @pl.when(jnp.logical_and(across, inner))
+        @pl.when(jnp.logical_and(jnp.logical_and(across, inner), side))
         def _():
             flush(relay.at[t, chunk(n)], qr.at[t, n])
-            acc[t, d, chunk(n)] += decode(relay[t, chunk(n)])
-            encode(t, chunk(n))
-            send(wire.at[t, chunk(n)], land.at[1, chunk(n)], gs, gr, (r, to, d)).start()
+            acc[t, d, chunk(n)] += relay[t, chunk(n)]
+            send(acc.at[t, d, chunk(n)], land.at[1, chunk(n)], gs, gr, (r, to, d)).start()
 
     deep, edge_chip = inner, jnp.logical_not(inner)
+    first = jnp.where(lax.div(r, 2) == lax.div(c, 2), 2, 1)
+    second = 3 - first
 
     def operator():
         load_pot.wait()
@@ -334,84 +321,90 @@
     operator()
     forwards(((1, 0), (3, 0), (2, 0), (1, 1), (2, 1), (1, 2), (2, 2)), ((1, 0), (3, 0), (2, 0), (3, 1), (1, 1), (3, 2)))
     tile(0, 0)
-    forwards(((1, 3), (2, 3)), ((1, 2), (1, 3)))
+    forwards(((1, 3), (2, 3)), ((1, 2), (1, 3), (1, 4)))
     settle(0, 0)
     far(0, 0)
-    near(0, 0, True)
+    near(0, 0)
     gathered(0)
     gathered(1)
     shared(0)
-    forwards((), ((3, 3),))
-    tile(2, 0)
-    forwards(((3, 1),), ((2, 1),))
-    tile(1, 0)
+    forwards(((1, 4), (2, 4)), ((3, 3), (3, 4)))
+    tile(first, 0)
+    forwards((), ((2, 1),))
+    tile(second, 0)
+    forwards(((3, 1),), ())
     swap(0)
-    settle(2, 0)
-    far(2, 0)
-    settle(1, 0)
-    far(1, 0)
-    near(2, 0, True)
-    near(1, 0, True)
+    settle(first, 0)
+    far(first, 0)
+    settle(second, 0)
+    far(second, 0)
+    near(2, 0)
+    near(1, 0)
     tile(0, 1)
     forwards(((3, 2),), ((2, 2),))
     settle(0, 1)
     far(0, 1)
-    near(0, 1, True)
+    near(0, 1)
+    forwards(((3, 3),), ((2, 3),))
+    gathered(2)
+    shared(1)
+    forwards(((3, 4),), ((2, 4),))
     swapped(0)
     far(3, 0)
-    near(3, 0, True)
-    gathered(2)
-    forwards(((3, 3),), ((2, 3),))
-    shared(1)
+    near(3, 0)
     pass_on(0, 0)
+    tile(first, 1)
     pass_on(2, 0)
-    tile(2, 1)
     pass_on(1, 0)
-    tile(1, 1)
+    tile(second, 1)
     swap(1)
-    settle(2, 1)
-    far(2, 1)
+    settle(first, 1)
+    far(first, 1)
+    pass_on(3, 0)
     pass_on(0, 1)
     tile(0, 2)
-    settle(1, 1)
-    far(1, 1)
-    near(2, 1, True)
-    near(1, 1, True)
-    pass_on(3, 0)
+    settle(second, 1)
+    far(second, 1)
+    near(2, 1, deep)
+    near(1, 1, deep)
     gathered(3)
     shared(2)
-    tile(2, 2)
+    swapped(1)
+    far(3, 1)
+    near(3, 1, deep)
+    tile(first, 2)
     settle(0, 2)
     far(0, 2)
     near(0, 2, deep)
-    swapped(1)
-    far(3, 1)
-    near(3, 1, deep)
-    pass_on(2, 1)
-    tile(1, 2)
-    pass_on(1, 1)
-    settle(2, 2)
-    far(2, 2)
-    near(2, 2, deep)
-    settle(1, 2)
-    far(1, 2)
-    near(1, 2, deep)
+    pass_on(first, 1)
+    tile(second, 2)
+    pass_on(second, 1)
+    settle(first, 2)
+    far(first, 2)
+    near(2, 2, jnp.logical_and(deep, first == 2))
+    near(1, 2, jnp.logical_and(deep, first == 1))
+    settle(second, 2)
+    far(second, 2)
+    near(2, 2, jnp.logical_and(deep, first == 1))
+    near(1, 2, jnp.logical_and(deep, first == 2))
+    pass_on(3, 1)
     near(3, 1, edge_chip)
+    near(2, 1, edge_chip)
     near(2, 2, edge_chip)
     pass_on(0, 2)
     pass_on(0, 3)
     swapped(2)
     far(3, 2)
-    near(3, 2, True)
+    near(3, 2)
+    near(1, 1, edge_chip)
     near(0, 2, edge_chip)
     near(1, 2, edge_chip)
-    pass_on(3, 1)
-    pass_on(2, 2)
-    pass_on(1, 2)
-    pass_on(2, 3)
-    pass_on(1, 3)
+    pass_on(first, 2)
+    pass_on(first, 3)
     pass_on(3, 2)
     pass_on(3, 3)
+    pass_on(second, 2)
+    pass_on(second, 3)
 
     flush(panel.at[0, 0:3], zs)
     flush(panel.at[0:2], xs)
@@ -421,7 +414,7 @@
     flush(cross, fs)
     mine = flip(r, c)
     flush(land, gr)
-    acc[mine, d] = (acc[mine, d] + decode(land[0]) + decode(land[1])) * dvol
+    acc[mine, d] = (acc[mine, d] + land[0] + land[1]) * dvol
     half, quad = wide // 2, wide // 8
     pick = lax.div(lane, quad)
     for a in range(GROUPS):
@@ -441,20 +434,20 @@
                             moved = pltpu.roll(total[b], (to - at) % wide, 1)
                             out = moved if out is None else jnp.where(pick == to // quad, moved, out)
                     rows = pl.ds(pl.multiple_of(first, size), size)
-                    inter[part, rows, pl.ds(v * wide, wide)] = out
+                    inter[rows, part, pl.ds(v * wide, wide)] = out
 
     flush(relay.at[0:3], gs)
 
 
-def publish(inter, applied, inter_out, applied_out, mixed, sems):
-    whole = pltpu.make_async_copy(applied, applied_out, sems.at[0])
-    whole.start()
-    for part in (0, 1):
-        mixed[:, part, :] = inter[part]
-    tiles = pltpu.make_async_copy(mixed, inter_out, sems.at[1])
-    tiles.start()
-    whole.wait()
-    tiles.wait()
+def publish(inter, applied, inter_out, applied_out, sems):
+    copies = [
+        pltpu.make_async_copy(applied, applied_out, sems.at[0]),
+        pltpu.make_async_copy(inter, inter_out, sems.at[1]),
+    ]
+    for cp in copies:
+        cp.start()
+    for cp in copies:
+        cp.wait()
 
 
 def stay(array):
@@ -476,7 +469,7 @@
     inter, applied = pl.pallas_call(
         functools.partial(kernel, dvol),
         out_shape=(
-            jax.ShapeDtypeStruct((2, half, rows), jnp.float32),
+            jax.ShapeDtypeStruct((half, 2, rows), jnp.float32),
             jax.ShapeDtypeStruct((parts, orbs, cells), jnp.bfloat16),
         ),
         in_specs=[pl.BlockSpec(memory_space=pltpu.HBM)] * 2,
@@ -490,11 +483,10 @@
             pltpu.VMEM((3,) + block, jnp.float32),
             pltpu.VMEM((2, 2, count, size, 8 * size), jnp.float32),
             pltpu.VMEM((2, 2, count - early, size, 8 * size), jnp.float32),
-            pltpu.VMEM((2, count, 3 * size, 8 * size), jnp.bfloat16),
-            pltpu.VMEM((4, count, 3 * size, 8 * size), jnp.bfloat16),
+            pltpu.VMEM((2,) + block, jnp.float32),
+            pltpu.VMEM((4,) + block, jnp.float32),
             pltpu.VMEM((2, early, size, 8 * size), jnp.float32),
-            pltpu.VMEM((4, count, 3 * size, 8 * size), jnp.bfloat16),
-            dma((2,)), dma, dma, dma, dma, dma((4, GROUPS)), dma, dma((GROUPS,)), dma, dma((3, steps)),
+            dma((2,)), dma, dma, dma, dma, dma((4, len(CUTS))), dma, dma((GROUPS,)), dma, dma((3, steps)),
             dma, dma, dma((4, pieces)), dma, dma((steps,)), dma, dma((steps,)), dma, dma,
         ],
         compiler_params=pltpu.CompilerParams(
@@ -510,7 +502,7 @@
         ),
         in_specs=[vmem, vmem],
         out_specs=[pl.BlockSpec(memory_space=pltpu.HBM)] * 2,
-        scratch_shapes=[pltpu.VMEM((half, 2, rows), jnp.float32), dma((2,))],
+        scratch_shapes=[dma((2,))],
         compiler_params=pltpu.CompilerParams(vmem_limit_bytes=16000000),
         name="publish",
     )(inter, applied)

time: 47.8 us -> 48.4 us (1.013)
  Pallas kernels: 46.7 us -> 47.3 us
    pallas_call x1, Pallas kernels: 45.6 us -> 46.3 us  [exchange(): pl.pallas_call(functools.partial(kernel, dvol), out_shape=(jax.ShapeDtype...]
where the time goes in v3:
time: 48.4 us; the launch traced here: 48 us
  Pallas kernels  47.3 us (98%)
  between operations  0.64 us (1%)
    pallas_call x1, Pallas kernels, exchange(): pl.pallas_call(functools.partial(kernel, dvol), out_shape=(jax.ShapeDtype...  46.3 us
    pallas_call x1, Pallas kernels, exchange(): pl.pallas_call(publish, out_shape=(jax.ShapeDtypeStruct((half, 2, rows),...  1.07 us

profile of v3, /device:TPU:6, one launch (start us, length us, event | category | flops | bytes accessed | tf_op | source)
XLA Modules:
  0.0 48.0 jit_solution(18273342842239374591)
XLA Ops:
  0.6 46.3 %overlap.1 = (f32[128,2,256]{2,1,0:T(2,128)S(1)}, bf16[2,64,4096]{2,1,0:T(8,128)(2,1)S(1)}) custom-call(bf16[2,64,4096]{2,1,0:T(8,128)(2,1)} %bitcast.4, f32[1,4096]{1,0:T(1,128)} %pot_hbm.1), custom_call_target="tpu_custom_call" | custom-call | tf_op jit(solution)/shard_map/overlap/pallas_call | solution.py:469
  46.9 1.1 %publish.1 = (f32[128,2,256]{2,1,0:T(2,128)}, bf16[2,64,4096]{2,1,0:T(8,128)(2,1)}) custom-call(f32[128,2,256]{2,1,0:T(2,128)S(1)} %get-tuple-element.6.inter, bf16[2,64,4096]{2,1,0:T(8,128)(2,1)S(1)} %get-tuple-element.7.applied), custom_call_target="tpu_custom_call" | custom-call | tf_op jit(solution)/shard_map/publish/pallas_call | solution.py:497

commit v4 on v3

--- a/solution.py
+++ b/solution.py
@@ -125,7 +125,7 @@
 
 
 def kernel(dvol, orb_hbm, pot_hbm, inter, applied, orb, pot, halo, panel, acc, take, pacc, cross,
-           land, relay, ptake, ins, hs, hr, ls, zs, zr, xs, xr, ds, dr, gs, gr, qr, rs, rr, ps, pr, fs, fr):
+           land, relay, ptake, wire, ins, hs, hr, ls, zs, zr, xs, xr, ds, dr, gs, gr, qr, rs, rr, ps, pr, fs, fr):
     r, c, d = lax.axis_index("row"), lax.axis_index("col"), lax.axis_index("depth")
     parts, orbs, cells = orb.shape
     quarter = cells // 4
@@ -275,6 +275,22 @@
             for j in (0, 1):
                 acc[3, d, span(s), pl.ds(j * size, size)] = cross[j, 0] + cross[j, 1]
 
+    def encode(t, blocks):
+        x = acc[t, d, blocks]
+        high = x.astype(jnp.bfloat16)
+        base = high.astype(jnp.float32)
+        steps = jnp.round((x - base) / jnp.maximum(jnp.abs(base), 1e-37) * 2048.0)
+        steps = jnp.clip(steps, -7.0, 7.0)
+        wire[t, blocks, :2 * size] = high
+        wire[t, blocks, 2 * size:] = (steps[:, :size] * 16.0 + steps[:, size:]).astype(jnp.bfloat16)
+
+    def decode(words):
+        base = words[:, :2 * size].astype(jnp.float32)
+        code = words[:, 2 * size:].astype(jnp.float32)
+        upper = jnp.round(code / 16.0)
+        steps = jnp.concatenate([upper, code - 16.0 * upper], axis=1)
+        return base + steps * jnp.abs(base) / 2048.0
+
     def route(t):
         to = flip(r, jnp.asarray(t, jnp.int32))
         return to, lax.div(to, 2) != lax.div(c, 2)
@@ -290,14 +306,16 @@
         def _():
             for n in range(len(PIECES)):
                 if PIECES[n][0] == s:
-                    send(acc.at[t, d, chunk(n)], relay.at[t, chunk(n)], gs, qr.at[t, n], zdev[1]).start()
+                    encode(t, chunk(n))
+                    send(wire.at[t, chunk(n)], relay.at[t, chunk(n)], gs, qr.at[t, n], zdev[1]).start()
 
     def near(t, s, side=True):
         to, across = route(t)
 
         @pl.when(jnp.logical_and(jnp.logical_and(to != c, jnp.logical_not(across)), side))
         def _():
-            send(acc.at[t, d, span(s)], land.at[0, span(s)], gs, gr, zdev[1]).start()
+            encode(t, span(s))
+            send(wire.at[t, span(s)], land.at[0, span(s)], gs, gr, zdev[1]).start()
 
     def pass_on(t, n, side=True):
         to, across = route(t)
@@ -305,8 +323,9 @@
         @pl.when(jnp.logical_and(jnp.logical_and(across, inner), side))
         def _():
             flush(relay.at[t, chunk(n)], qr.at[t, n])
-            acc[t, d, chunk(n)] += relay[t, chunk(n)]
-            send(acc.at[t, d, chunk(n)], land.at[1, chunk(n)], gs, gr, (r, to, d)).start()
+            acc[t, d, chunk(n)] += decode(relay[t, chunk(n)])
+            encode(t, chunk(n))
+            send(wire.at[t, chunk(n)], land.at[1, chunk(n)], gs, gr, (r, to, d)).start()
 
     deep, edge_chip = inner, jnp.logical_not(inner)
     first = jnp.where(lax.div(r, 2) == lax.div(c, 2), 2, 1)
@@ -346,16 +365,16 @@
     far(0, 1)
     near(0, 1)
     forwards(((3, 3),), ((2, 3),))
+    pass_on(0, 0)
     gathered(2)
+    pass_on(first, 0)
     shared(1)
     forwards(((3, 4),), ((2, 4),))
     swapped(0)
     far(3, 0)
     near(3, 0)
-    pass_on(0, 0)
     tile(first, 1)
-    pass_on(2, 0)
-    pass_on(1, 0)
+    pass_on(second, 0)
     tile(second, 1)
     swap(1)
     settle(first, 1)
@@ -369,13 +388,13 @@
     near(1, 1, deep)
     gathered(3)
     shared(2)
+    settle(0, 2)
+    far(0, 2)
+    near(0, 2, deep)
     swapped(1)
     far(3, 1)
     near(3, 1, deep)
     tile(first, 2)
-    settle(0, 2)
-    far(0, 2)
-    near(0, 2, deep)
     pass_on(first, 1)
     tile(second, 2)
     pass_on(second, 1)
@@ -414,7 +433,7 @@
     flush(cross, fs)
     mine = flip(r, c)
     flush(land, gr)
-    acc[mine, d] = (acc[mine, d] + land[0] + land[1]) * dvol
+    acc[mine, d] = (acc[mine, d] + decode(land[0]) + decode(land[1])) * dvol
     half, quad = wide // 2, wide // 8
     pick = lax.div(lane, quad)
     for a in range(GROUPS):
@@ -465,6 +484,7 @@
     vmem = pl.BlockSpec(memory_space=pltpu.VMEM)
     dma = pltpu.SemaphoreType.DMA
     block = (count, 2 * size, 8 * size)
+    words = (count, 3 * size, 8 * size)
     early = blocks()[1][-1][0]
     inter, applied = pl.pallas_call(
         functools.partial(kernel, dvol),
@@ -483,9 +503,10 @@
             pltpu.VMEM((3,) + block, jnp.float32),
             pltpu.VMEM((2, 2, count, size, 8 * size), jnp.float32),
             pltpu.VMEM((2, 2, count - early, size, 8 * size), jnp.float32),
-            pltpu.VMEM((2,) + block, jnp.float32),
-            pltpu.VMEM((4,) + block, jnp.float32),
+            pltpu.VMEM((2,) + words, jnp.bfloat16),
+            pltpu.VMEM((4,) + words, jnp.bfloat16),
             pltpu.VMEM((2, early, size, 8 * size), jnp.float32),
+            pltpu.VMEM((4,) + words, jnp.bfloat16),
             dma((2,)), dma, dma, dma, dma, dma((4, len(CUTS))), dma, dma((GROUPS,)), dma, dma((3, steps)),
             dma, dma, dma((4, pieces)), dma, dma((steps,)), dma, dma((steps,)), dma, dma,
         ],

time: 48.4 us -> 46.5 us (0.961)
  Pallas kernels: 47.3 us -> 45.7 us
    pallas_call x1, Pallas kernels: 46.3 us -> 44.6 us  [exchange(): pl.pallas_call(functools.partial(kernel, dvol), out_shape=(jax.ShapeDtype...]
where the time goes in v4:
time: 46.5 us; the launch traced here: 46.3 us
  Pallas kernels  45.7 us (98%)
  between operations  0.64 us (1%)
    pallas_call x1, Pallas kernels, exchange(): pl.pallas_call(functools.partial(kernel, dvol), out_shape=(jax.ShapeDtype...  44.6 us
    pallas_call x1, Pallas kernels, exchange(): pl.pallas_call(publish, out_shape=(jax.ShapeDtypeStruct((half, 2, rows),...  1.07 us

profile of v4, /device:TPU:6, one launch (start us, length us, event | category | flops | bytes accessed | tf_op | source)
XLA Modules:
  0.0 46.3 jit_solution(11825772658851182401)
XLA Ops:
  0.6 44.6 %overlap.1 = (f32[128,2,256]{2,1,0:T(2,128)S(1)}, bf16[2,64,4096]{2,1,0:T(8,128)(2,1)S(1)}) custom-call(bf16[2,64,4096]{2,1,0:T(8,128)(2,1)} %bitcast.4, f32[1,4096]{1,0:T(1,128)} %pot_hbm.1), custom_call_target="tpu_custom_call" | custom-call | tf_op jit(solution)/shard_map/overlap/pallas_call | solution.py:489
  45.3 1.1 %publish.1 = (f32[128,2,256]{2,1,0:T(2,128)}, bf16[2,64,4096]{2,1,0:T(8,128)(2,1)}) custom-call(f32[128,2,256]{2,1,0:T(2,128)S(1)} %get-tuple-element.6.inter, bf16[2,64,4096]{2,1,0:T(8,128)(2,1)S(1)} %get-tuple-element.7.applied), custom_call_target="tpu_custom_call" | custom-call | tf_op jit(solution)/shard_map/publish/pallas_call | solution.py:518

commit v5 on v3

--- a/solution.py
+++ b/solution.py
@@ -346,16 +346,16 @@
     far(0, 1)
     near(0, 1)
     forwards(((3, 3),), ((2, 3),))
+    pass_on(0, 0)
     gathered(2)
+    pass_on(first, 0)
     shared(1)
     forwards(((3, 4),), ((2, 4),))
     swapped(0)
     far(3, 0)
     near(3, 0)
-    pass_on(0, 0)
     tile(first, 1)
-    pass_on(2, 0)
-    pass_on(1, 0)
+    pass_on(second, 0)
     tile(second, 1)
     swap(1)
     settle(first, 1)
@@ -369,13 +369,13 @@
     near(1, 1, deep)
     gathered(3)
     shared(2)
+    settle(0, 2)
+    far(0, 2)
+    near(0, 2, deep)
     swapped(1)
     far(3, 1)
     near(3, 1, deep)
     tile(first, 2)
-    settle(0, 2)
-    far(0, 2)
-    near(0, 2, deep)
     pass_on(first, 1)
     tile(second, 2)
     pass_on(second, 1)

time: 48.4 us -> 48.4 us (level)
  no operation moved by 1% of the time
where the time goes in v5:
time: 48.4 us; the launch traced here: 48 us
  Pallas kernels  47.4 us (98%)
  between operations  0.64 us (1%)
    pallas_call x1, Pallas kernels, exchange(): pl.pallas_call(functools.partial(kernel, dvol), out_shape=(jax.ShapeDtype...  46.3 us
    pallas_call x1, Pallas kernels, exchange(): pl.pallas_call(publish, out_shape=(jax.ShapeDtypeStruct((half, 2, rows),...  1.07 us

profile of v5, /device:TPU:6, one launch (start us, length us, event | category | flops | bytes accessed | tf_op | source)
XLA Modules:
  0.0 48.0 jit_solution(15741438582169884779)
XLA Ops:
  0.6 46.3 %overlap.1 = (f32[128,2,256]{2,1,0:T(2,128)S(1)}, bf16[2,64,4096]{2,1,0:T(8,128)(2,1)S(1)}) custom-call(bf16[2,64,4096]{2,1,0:T(8,128)(2,1)} %bitcast.4, f32[1,4096]{1,0:T(1,128)} %pot_hbm.1), custom_call_target="tpu_custom_call" | custom-call | tf_op jit(solution)/shard_map/overlap/pallas_call | solution.py:469
  46.9 1.1 %publish.1 = (f32[128,2,256]{2,1,0:T(2,128)}, bf16[2,64,4096]{2,1,0:T(8,128)(2,1)}) custom-call(f32[128,2,256]{2,1,0:T(2,128)S(1)} %get-tuple-element.6.inter, bf16[2,64,4096]{2,1,0:T(8,128)(2,1)S(1)} %get-tuple-element.7.applied), custom_call_target="tpu_custom_call" | custom-call | tf_op jit(solution)/shard_map/publish/pallas_call | solution.py:497

commit v6 on v4

--- a/solution.py
+++ b/solution.py
@@ -99,7 +99,7 @@
 
 
 STAGES = ((0, 2), (2, 3), (3, 4))
-PIECES = ((0, 0, 4), (1, 0, 5), (2, 0, 4), (2, 4, 3))
+PIECES = ((0, 0, 4), (1, 0, 5), (2, 0, 3), (2, 3, 2), (2, 5, 2))
 GROUPS = 4
 OUTER, INNER = 0, 1
 MEMBERS = (
@@ -267,9 +267,11 @@
             dst = acc.at[3, d, span(s), pl.ds((j - 1) * size, size)]
             send(pacc.at[d, j - 1, span(s)], dst, rs, rr.at[s], xdev[j]).start()
 
-    def swapped(s):
+    def swapped(s, side=True):
         if s < last:
-            flush(acc.at[3, d, span(s)], rr.at[s])
+            @pl.when(side)
+            def _():
+                flush(acc.at[3, d, span(s)], rr.at[s])
         else:
             flush(cross, fr)
             for j in (0, 1):
@@ -391,10 +393,12 @@
     settle(0, 2)
     far(0, 2)
     near(0, 2, deep)
-    swapped(1)
+    swapped(1, first == 2)
     far(3, 1)
-    near(3, 1, deep)
+    near(3, 1, jnp.logical_and(deep, first == 2))
     tile(first, 2)
+    swapped(1, first == 1)
+    near(3, 1, jnp.logical_and(deep, first == 1))
     pass_on(first, 1)
     tile(second, 2)
     pass_on(second, 1)
@@ -410,20 +414,20 @@
     near(3, 1, edge_chip)
     near(2, 1, edge_chip)
     near(2, 2, edge_chip)
-    pass_on(0, 2)
-    pass_on(0, 3)
+    for n in (2, 3, 4):
+        pass_on(0, n)
     swapped(2)
     far(3, 2)
     near(3, 2)
     near(1, 1, edge_chip)
     near(0, 2, edge_chip)
     near(1, 2, edge_chip)
-    pass_on(first, 2)
-    pass_on(first, 3)
-    pass_on(3, 2)
-    pass_on(3, 3)
-    pass_on(second, 2)
-    pass_on(second, 3)
+    for n in (2, 3, 4):
+        pass_on(first, n)
+    for n in (2, 3, 4):
+        pass_on(3, n)
+    for n in (2, 3, 4):
+        pass_on(second, n)
 
     flush(panel.at[0, 0:3], zs)
     flush(panel.at[0:2], xs)

time: 46.5 us -> 46.5 us (level)
  no operation moved by 1% of the time
where the time goes in v6:
time: 46.5 us; the launch traced here: 46.4 us
  Pallas kernels  45.7 us (98%)
  between operations  0.64 us (1%)
    pallas_call x1, Pallas kernels, exchange(): pl.pallas_call(functools.partial(kernel, dvol), out_shape=(jax.ShapeDtype...  44.7 us
    pallas_call x1, Pallas kernels, exchange(): pl.pallas_call(publish, out_shape=(jax.ShapeDtypeStruct((half, 2, rows),...  1.07 us

profile of v6, /device:TPU:6, one launch (start us, length us, event | category | flops | bytes accessed | tf_op | source)
XLA Modules:
  0.0 46.4 jit_solution(1004087771680535334)
XLA Ops:
  0.6 44.7 %overlap.1 = (f32[128,2,256]{2,1,0:T(2,128)S(1)}, bf16[2,64,4096]{2,1,0:T(8,128)(2,1)S(1)}) custom-call(bf16[2,64,4096]{2,1,0:T(8,128)(2,1)} %bitcast.4, f32[1,4096]{1,0:T(1,128)} %pot_hbm.1), custom_call_target="tpu_custom_call" | custom-call | tf_op jit(solution)/shard_map/overlap/pallas_call | solution.py:493
  45.3 1.1 %publish.1 = (f32[128,2,256]{2,1,0:T(2,128)}, bf16[2,64,4096]{2,1,0:T(8,128)(2,1)}) custom-call(f32[128,2,256]{2,1,0:T(2,128)S(1)} %get-tuple-element.6.inter, bf16[2,64,4096]{2,1,0:T(8,128)(2,1)S(1)} %get-tuple-element.7.applied), custom_call_target="tpu_custom_call" | custom-call | tf_op jit(solution)/shard_map/publish/pallas_call | solution.py:522
